TPU v7x, 32 devices: a whole 2x2x4 slice. The times are simulated.
32 devices in a mesh: section: 2 (over x), expert: 16 (over z, y, core).
Axes of the slice: x: 2, y: 2, z: 4, core: 2. Of those that a mesh axis runs over, the one named last changes fastest.
Arguments:
- images: bfloat16 [32, 256, 1408], P(('section', 'expert')), may hold values from -6 to 6
- norm_gain: bfloat16 [1408], replicated, may hold values from 0.5 to 1.5
- slot_map: bfloat16 [1408, 16], replicated, may hold values from -0.15625 to 0.15625
- logit_scale: float32 [1], replicated, may hold values from 30 to 80
- up_weight: bfloat16 [16, 5120, 1408], P('expert', 'section'), may hold values from -0.625 to 0.625
- down_weight: bfloat16 [16, 5120, 1408], P('expert', 'section'), may hold values from -0.3125 to 0.3125
Outputs:
- block_out: bfloat16 [32, 256, 1408], P(('section', 'expert'))
All inputs are finite; a program needn't handle non-finite values.
Results may differ from a plain program's by a relative error of at most 0.011.
Values may be sent and summed in bfloat16 or wider, within the bound.
No kernel may reach another device: no remote copies, remote signals or barrier semaphores. Data moves between devices by JAX's collectives and lax.ppermute only.
A program may use at most 64 MiB of HBM per device.

v0:
```python
import jax
import jax.numpy as jnp
from jax import lax
from jax.sharding import PartitionSpec as P

epsilon = 1e-06


def normalize(inputs, gain_row):
    values = inputs.astype(jnp.float32)
    spread = jnp.mean(values * values, axis=-1, keepdims=True)
    return (values * lax.rsqrt(spread + epsilon) * gain_row.astype(jnp.float32)).astype(
        jnp.bfloat16
    )


def weights_from(raw, normed, slot_cols, scale_now):
    values = normed.astype(jnp.float32)
    token_norm = jnp.sqrt(jnp.sum(values * values, axis=-1) + epsilon)
    columns = slot_cols.astype(jnp.float32)
    column_norm = jnp.sqrt(jnp.sum(columns * columns, axis=0) + epsilon)
    logits = scale_now * raw / (token_norm[:, None, :] * column_norm[None, :, None])
    scores = jnp.exp(logits)
    dispatch = (scores / jnp.sum(scores, axis=-1, keepdims=True)).astype(jnp.bfloat16)
    combine = (scores / jnp.sum(scores, axis=1, keepdims=True)).astype(jnp.bfloat16)
    return (dispatch, combine)


def local(images, norm_gain, slot_map, logit_scale, up_weight, down_weight):
    position = lax.axis_index("section")
    normed = normalize(images, norm_gain)
    raw = jnp.einsum("itd,de->iet", normed, slot_map, preferred_element_type=jnp.float32)
    dispatch, combine = weights_from(raw, normed, slot_map, logit_scale[0])
    slot_in = jnp.einsum(
        "iet,itd->eid", dispatch, normed, preferred_element_type=jnp.float32
    ).astype(jnp.bfloat16)
    slots = lax.all_to_all(slot_in, "expert", split_axis=0, concat_axis=1, tiled=True)
    count = slots.shape[1]
    gathered = lax.all_gather(slots, "section", axis=1, tiled=True)
    hidden = jax.nn.gelu(
        jnp.einsum("esd,efd->esf", gathered, up_weight, preferred_element_type=jnp.float32)
    ).astype(jnp.bfloat16)
    partial_sum = jnp.einsum(
        "esf,efd->esd", hidden, down_weight, preferred_element_type=jnp.float32
    )
    totals = lax.psum(partial_sum, "section")
    own_rows = lax.dynamic_slice_in_dim(totals, position * count, count, 1)
    result = own_rows.astype(jnp.bfloat16)
    back = lax.all_to_all(result, "expert", split_axis=1, concat_axis=0, tiled=True)
    mixed = jnp.einsum("iet,eid->itd", combine, back, preferred_element_type=jnp.float32)
    return (images.astype(jnp.float32) + mixed).astype(jnp.bfloat16)


def solution(mesh):
    return jax.shard_map(
        local,
        mesh=mesh,
        in_specs=(
            P(("section", "expert"), None, None),
            P(),
            P(),
            P(),
            P("expert", "section", None),
            P("expert", "section", None),
        ),
        out_specs=P(("section", "expert"), None, None),
        check_vma=False,
    )
```

profile of v0, /device:TPU:0, one launch (start us, length us, event | category | flops | bytes accessed | tf_op | source)
XLA Modules:
  0.0 58.3 jit_solution(4352403339752684257)
XLA Ops:
  0.0 0.0 copy-start.1
  0.7 0.9 %multiply_reduce_fusion.1 = f32[16]{0:T(128)S(1)} fusion(bf16[1408,16]{0,1:T(8,128)(2,1)} %param.8), kind=kLoop, calls=%fused_computation.37 | loop fusion | flops 67568 | bytes 45120 | tf_op jit(solution)/shard_map/reduce_sum | solution.py:21
  1.6 1.3 %fusion.10 = f32[256]{0:T(256)S(1)} fusion(bf16[1,256,1408]{2,1,0:T(8,128)(2,1)} %param.6), kind=kLoop, calls=%fused_computation.12 | loop fusion | flops 1081088 | bytes 721920 | tf_op jit(solution)/shard_map/reduce_sum | solution.py:11
  3.0 0.7 %convert_element_type.44 = f32[1408]{0:T(1024)S(1)} convert(bf16[1408]{0:T(1024)(128)(2,1)} %param.7) | non-fusion elementwise | flops 1408 | bytes 8448 | tf_op jit(solution)/shard_map/convert_element_type | solution.py:12
  3.7 1.5 %multiply_reduce_fusion = f32[256]{0:T(256)S(1)} fusion(f32[1408]{0:T(1024)S(1)} %convert_element_type.44, f32[256]{0:T(256)S(1)} %add_rsqrt_fusion, bf16[1,256,1408]{2,1,0:T(8,128)(2,1)} %param.6), kind=kLoop, calls=%fused_computation.15 | loop fusion | flops 2522880 | bytes 728576 | tf_op jit(solution)/shard_map/reduce_sum | solution.py:19
  5.2 0.0 copy-done.1
  5.2 0.0 copy-done
  5.2 0.5 fusion.48
  5.7 0.4 fusion.9
  6.1 0.6 %broadcast.46 = bf16[]{:T(256)} broadcast(bf16[]{:T(256)} %constant.65), dimensions={} | broadcast | bytes 4 | tf_op jit(solution)/shard_map/convert_element_type | solution.py:36
  6.7 0.7 %reduce.6 = bf16[16,1408]{1,0:T(8,128)(2,1)S(1)} reduce(bf16[16,1,1408]{2,0,1:T(8,128)(2,1)S(1)} %fusion.9, bf16[]{:T(256)} %broadcast.46), dimensions={1}, to_apply=%copy.9.reduce_sub_computation | reduce | bytes 90114 | tf_op jit(solution)/shard_map/convert_element_type | solution.py:36
  7.4 0.7 %reshape.104 = bf16[16,2,704]{2,1,0:T(2,128)(2,1)} reshape(bf16[16,1408]{1,0:T(8,128)(2,1)S(1)} %reduce.6) | data formatting | bytes 90112
  8.1 7.4 %all-to-all-start = ((bf16[16,2,704]{2,1,0:T(2,128)(2,1)}), bf16[16,2,704]{2,1,0:T(2,128)(2,1)S(1)}, u32[]{:S(2)}, u32[]{:S(2)}) async-start(bf16[16,2,704]{2,1,0:T(2,128)(2,1)} %reshape.104), calls=%async_computation | async-start | bytes 98304 | tf_op jit(solution)/shard_map/all_to_all | solution.py:37
  15.5 6.8 %all-to-all-done = bf16[16,2,704]{2,1,0:T(2,128)(2,1)S(1)} async-done(((bf16[16,2,704]{2,1,0:T(2,128)(2,1)}), bf16[16,2,704]{2,1,0:T(2,128)(2,1)S(1)}, u32[]{:S(2)}, u32[]{:S(2)}) %all-to-all-start) | async-done | bytes 45088 | tf_op jit(solution)/shard_map/all_to_all | solution.py:37
  22.3 0.1 reshape.105
  22.4 4.7 %all-gather = bf16[32,1,1408]{2,0,1:T(8,128)(2,1)S(1)} all-gather(bf16[16,1,1408]{2,0,1:T(8,128)(2,1)S(1)} %copy.10), channel_id=2, replica_groups=mesh['section'=2,'expert'=16] {'section'}, dimensions={0}, use_global_device_ids=true | all-gather | bytes 135168 | tf_op jit(solution)/shard_map/all_gather | solution.py:39
  27.2 8.4 %fusion.6 = f32[1,32,1408]{2,1,0:T(8,128)S(1)} fusion(bf16[1,2560,1408]{2,1,0:T(8,128)(2,1)} %param.11, bf16[1,2560,1408]{2,1,0:T(8,128)(2,1)} %param.10, bf16[32,1,1408]{2,0,1:T(8,128)(2,1)S(1)} %all-gather), kind=kOutput, calls=%fused_computation.7 | convolution fusion | flops 462110720 | bytes 14688256 | tf_op jit(solution)/shard_map/esf,efd->esd/dot_general | solution.py:43
  35.6 10.9 %all-reduce.1 = bf16[1,32,1408]{2,1,0:T(8,128)(2,1)S(1)} all-reduce(f32[1,32,1408]{2,1,0:T(8,128)S(1)} %fusion.6), channel_id=1, replica_groups=mesh['section'=2,'expert'=16] {'section'}, use_global_device_ids=true, to_apply=%region_5.0 | all-reduce | flops 45056 | bytes 270336 | tf_op jit(solution)/shard_map/psum | solution.py:46
  46.5 0.1 copy.18
  46.6 0.9 %reduce.7 = bf16[16,1408]{1,0:T(8,128)(2,1)S(1)} reduce(bf16[16,1,1408]{2,1,0:T(2,128)(2,1)S(1)} %bitcast.53, bf16[]{:T(256)} %broadcast.46), dimensions={1}, to_apply=%bitcast.51.reduce_sub_computation | reduce | bytes 90114
  47.5 0.1 reshape.106
  47.6 9.3 %all_to_all.21 = bf16[16,2,704]{2,1,0:T(2,128)(2,1)S(1)} all-to-all(bf16[16,2,704]{2,1,0:T(2,128)(2,1)S(1)} %reshape.106), channel_id=1, replica_groups=mesh['section'=2,'expert'=16] {'expert'}, dimensions={0} | all-to-all | bytes 90112 | tf_op jit(solution)/shard_map/all_to_all | solution.py:49
  57.0 0.1 reshape.107
  57.1 1.3 %fusion.5 = bf16[1,256,1408]{2,1,0:T(8,128)(2,1)} fusion(bf16[1,256,1408]{2,1,0:T(8,128)(2,1)S(1)} %copy-done, bf16[1,16,1408]{2,0,1:T(2,128)(2,1)S(1)} %bitcast.54, f32[16,256]{1,0:T(8,128)S(1)} %get-tuple-element.7, f32[256]{0:T(256)S(1)} %get-tuple-element.5), kind=kOutput, calls=%fused_computation.6 | convolution fusion | flops 12623872 | bytes 1504256 | tf_op jit(solution)/shard_map/iet,eid->itd/dot_general | solution.py:50
  (6 shorter events, 0.1 us)
Async XLA Ops:
  0.0 5.2 %copy-start.1 = (bf16[1408,16]{0,1:T(8,128)(2,1)S(1)}, bf16[1408,16]{0,1:T(8,128)(2,1)}, u32[]{:S(2)}) copy-start(bf16[1408,16]{0,1:T(8,128)(2,1)} %param.8) | copy-start | bytes 135172
  0.0 5.2 %copy-start = (bf16[1,256,1408]{2,1,0:T(8,128)(2,1)S(1)}, bf16[1,256,1408]{2,1,0:T(8,128)(2,1)}, u32[]{:S(2)}) copy-start(bf16[1,256,1408]{2,1,0:T(8,128)(2,1)} %param.6) | copy-start | bytes 2162692
  8.1 14.2 %all-to-all-start = ((bf16[16,2,704]{2,1,0:T(2,128)(2,1)}), bf16[16,2,704]{2,1,0:T(2,128)(2,1)S(1)}, u32[]{:S(2)}, u32[]{:S(2)}) async-start(bf16[16,2,704]{2,1,0:T(2,128)(2,1)} %reshape.104), calls=%async_computation | async-start | bytes 98304 | tf_op jit(solution)/shard_map/all_to_all | solution.py:37
where the time goes:
time: 58.8 us; the launch traced here: 58.3 us
  blocking collectives  24.9 us (42%)
  matrix products  10.6 us (18%)
  starting transfers between devices  7.41 us (13%)
  waiting for transfers between devices  6.76 us (11%)
  other arithmetic  6.08 us (10%)
  local copies, waits for them, and re-layouts  1.79 us (3%)
  between operations  0.82 us (1%)
    psum x1, blocking collectives, local(): totals = lax.psum(partial_sum, 'section')  10.9 us
    all_to_all x1, blocking collectives, local(): lax.all_to_all(result, 'expert', split_axis=1, concat_axis=0, tiled=True)  9.34 us
    dot_general x1, matrix products, local(): jnp.einsum('esf,efd->esd', hidden, down_weight, preferred_element_type=jn...  8.44 us
    all_to_all x1, starting transfers between devices, local(): lax.all_to_all(slot_in, 'expert', split_axis=0, concat_axis=1, tiled=True)  7.41 us
    all_to_all x1, waiting for transfers between devices, local(): lax.all_to_all(slot_in, 'expert', split_axis=0, concat_axis=1, tiled=True)  6.76 us
    all_gather x1, blocking collectives, local(): gathered = lax.all_gather(slots, 'section', axis=1, tiled=True)  4.71 us
    reduce_sum x1, other arithmetic, weights_from(): token_norm = jnp.sqrt(jnp.sum(values * values, axis=-1) + epsilon)  1.48 us
    reduce_sum x1, other arithmetic, normalize(): spread = jnp.mean(values * values, axis=-1, keepdims=True)  1.34 us
  transfers between devices with their start and end apart: 1, of which 1 were waited for; matrix products, arithmetic and copies ran while one was open for 0% of the time, Pallas kernels for 0%

commit v1 on v0

v1 whole, which is shorter than its diff:
```python
import jax
import jax.numpy as jnp
from jax import lax
from jax.experimental import pallas as pl
from jax.experimental.pallas import tpu as pltpu
from jax.sharding import PartitionSpec as P

epsilon = 1e-06
LANES = 128
f32 = jnp.float32
bf16 = jnp.bfloat16
NT = (((1,), (1,)), ((), ()))
TN = (((0,), (0,)), ((), ()))


def packed_rows(width):
    return -(-(width // LANES) // 16) * 16


def to_pieces(values, flat_ref, piece_ref, copies):
    count, width = values.shape
    rows = piece_ref.shape[1]
    flat_ref[...] = jnp.zeros(flat_ref.shape, f32)
    for j in range(width // LANES):
        flat_ref[pl.ds(j, count, stride=rows), :] = values[:, j * LANES : (j + 1) * LANES]
    pieces = flat_ref[...].astype(bf16).reshape(count, rows, LANES)
    for c in range(copies):
        piece_ref[c * count : (c + 1) * count] = pieces


def from_pieces(piece_ref, flat_ref, width):
    count, rows, _ = piece_ref.shape
    flat_ref[...] = piece_ref[...].reshape(count * rows, LANES).astype(f32)
    parts = [flat_ref[pl.ds(j, count, stride=rows), :] for j in range(width // LANES)]
    return jnp.concatenate(parts, axis=1).astype(bf16)


def routing_kernel(scale_ref, images_ref, gain_ref, slots_ref, piece_ref, combine_ref, flat_ref, *, sections):
    values = images_ref[...].astype(f32)
    spread = jnp.mean(values * values, axis=-1, keepdims=True)
    normed = (values * lax.rsqrt(spread + epsilon) * gain_ref[...].astype(f32)).astype(bf16)
    slot_rows = slots_ref[...]
    raw = lax.dot_general(normed, slot_rows, NT, preferred_element_type=f32)
    wide = normed.astype(f32)
    token_norm = jnp.sqrt(jnp.sum(wide * wide, axis=-1, keepdims=True) + epsilon)
    columns = slot_rows.astype(f32)
    column_norm = jnp.sqrt(jnp.sum(columns * columns, axis=-1, keepdims=True) + epsilon)
    count = slot_rows.shape[0]
    column_row = jnp.transpose(jnp.broadcast_to(column_norm, (count, LANES)))[:1, :]
    scores = jnp.exp(scale_ref[0] * raw / (token_norm * column_row))
    dispatch = (scores / jnp.sum(scores, axis=0, keepdims=True)).astype(bf16)
    slot_in = lax.dot_general(dispatch, normed, TN, preferred_element_type=f32)
    to_pieces(slot_in, flat_ref, piece_ref, sections)
    combine = (scores / jnp.sum(scores, axis=1, keepdims=True)).astype(bf16)
    combine_ref[...] = jnp.concatenate([combine] * sections, axis=1)


def routing(scale, images, gain, slot_rows, sections):
    tokens, width = images.shape
    count = slot_rows.shape[0]
    rows = packed_rows(width)
    vmem = pl.BlockSpec(memory_space=pltpu.VMEM)
    return pl.pallas_call(
        lambda *refs: routing_kernel(*refs, sections=sections),
        out_shape=(
            jax.ShapeDtypeStruct((sections * count, rows, LANES), bf16),
            jax.ShapeDtypeStruct((tokens, sections * count), bf16),
        ),
        in_specs=[pl.BlockSpec(memory_space=pltpu.SMEM), vmem, vmem, vmem],
        out_specs=(vmem, vmem),
        scratch_shapes=[pltpu.VMEM((count * rows, LANES), f32)],
        name="routing",
    )(scale, images, gain, slot_rows)


def experts_kernel(piece_ref, up_hbm, down_hbm, out_ref, up_ref, down_ref, flat_ref, sems, *, chunk):
    hidden_rows, width = up_ref.shape
    steps = hidden_rows // chunk

    def copies(i):
        part = pl.ds(i * chunk, chunk)
        return (
            pltpu.make_async_copy(up_hbm.at[part], up_ref.at[part], sems.at[0, i]),
            pltpu.make_async_copy(down_hbm.at[part], down_ref.at[part], sems.at[1, i]),
        )

    for i in range(steps):
        for copy in copies(i):
            copy.start()
    inputs = from_pieces(piece_ref, flat_ref, width)
    total = None
    for i in range(steps):
        up_copy, down_copy = copies(i)
        up_copy.wait()
        part = slice(i * chunk, (i + 1) * chunk)
        hidden = lax.dot_general(inputs, up_ref[part, :], NT, preferred_element_type=f32)
        hidden = jax.nn.gelu(hidden).astype(bf16)
        down_copy.wait()
        term = jnp.dot(hidden, down_ref[part, :], preferred_element_type=f32)
        total = term if total is None else total + term
    to_pieces(total, flat_ref, out_ref, 1)


def experts(pieces, up, down):
    hidden_rows, width = up.shape
    count, rows, _ = pieces.shape
    chunk = next(c for c in (512, 256, 128, hidden_rows) if hidden_rows % c == 0)
    steps = hidden_rows // chunk
    vmem = pl.BlockSpec(memory_space=pltpu.VMEM)
    anywhere = pl.BlockSpec(memory_space=pl.ANY)
    return pl.pallas_call(
        lambda *refs: experts_kernel(*refs, chunk=chunk),
        out_shape=jax.ShapeDtypeStruct(pieces.shape, bf16),
        in_specs=[vmem, anywhere, anywhere],
        out_specs=vmem,
        scratch_shapes=[
            pltpu.VMEM((hidden_rows, width), bf16),
            pltpu.VMEM((hidden_rows, width), bf16),
            pltpu.VMEM((count * rows, LANES), f32),
            pltpu.SemaphoreType.DMA((2, steps)),
        ],
        name="experts",
    )(pieces, up, down)


def mixing_kernel(images_ref, combine_ref, piece_ref, out_ref, flat_ref):
    outputs = from_pieces(piece_ref, flat_ref, images_ref.shape[1])
    mixed = jnp.dot(combine_ref[...], outputs, preferred_element_type=f32)
    out_ref[...] = (images_ref[...].astype(f32) + mixed).astype(bf16)


def mixing(images, combine, pieces):
    count, rows, _ = pieces.shape
    vmem = pl.BlockSpec(memory_space=pltpu.VMEM)
    return pl.pallas_call(
        mixing_kernel,
        out_shape=jax.ShapeDtypeStruct(images.shape, bf16),
        in_specs=[vmem, vmem, vmem],
        out_specs=vmem,
        scratch_shapes=[pltpu.VMEM((count * rows, LANES), f32)],
        name="mixing",
    )(images, combine, pieces)


def exchange(pieces):
    return lax.all_to_all(pieces, ("section", "expert"), split_axis=0, concat_axis=0, tiled=True)


def solution(mesh):
    sections = mesh.shape["section"]

    def local(images, norm_gain, slot_map, logit_scale, up_weight, down_weight):
        own = images[0]
        pieces, combine = routing(logit_scale, own, norm_gain[None, :], slot_map.T, sections)
        arrived = exchange(pieces)
        results = experts(arrived, up_weight[0], down_weight[0])
        back = exchange(results)
        return mixing(own, combine, back)[None]

    return jax.shard_map(
        local,
        mesh=mesh,
        in_specs=(
            P(("section", "expert"), None, None),
            P(),
            P(),
            P(),
            P("expert", "section", None),
            P("expert", "section", None),
        ),
        out_specs=P(("section", "expert"), None, None),
        check_vma=False,
    )
```

time: 58.8 us -> 42.1 us (0.72)
  Pallas kernels: 0 us -> 12.7 us
  matrix products: 10.6 us -> 0 us
  starting transfers between devices: 7.41 us -> 0 us
  waiting for transfers between devices: 6.76 us -> 0 us
  other arithmetic: 6.08 us -> 0 us
  blocking collectives: 24.9 us -> 27.1 us
    all_to_all x1 -> x2, blocking collectives: 9.34 us -> 27.1 us  [exchange(): lax.all_to_all(pieces, ('section', 'expert'), split_axis=0, concat_axis=0...]
    pallas_call x0 -> x3, Pallas kernels: none -> 12.7 us  [the longest x1 7.57 us: experts(): pl.pallas_call(lambda *refs: experts_kernel(*refs, chunk=chunk), out_shap...]
    psum x1 -> x0, blocking collectives: 10.9 us -> none  [local(): totals = lax.psum(partial_sum, 'section')]
    dot_general x4 -> x0, matrix products: 10.6 us -> none  [the longest x1 8.44 us: local(): jnp.einsum('esf,efd->esd', hidden, down_weight, preferred_element_type=jn...]
    all_to_all x1 -> x0, starting transfers between devices: 7.41 us -> none  [local(): lax.all_to_all(slot_in, 'expert', split_axis=0, concat_axis=1, tiled=True)]
    all_to_all x1 -> x0, waiting for transfers between devices: 6.76 us -> none  [local(): lax.all_to_all(slot_in, 'expert', split_axis=0, concat_axis=1, tiled=True)]
    all_gather x1 -> x0, blocking collectives: 4.71 us -> none  [local(): gathered = lax.all_gather(slots, 'section', axis=1, tiled=True)]
    reduce_sum x3 -> x0, other arithmetic: 3.73 us -> none  [the longest x1 1.48 us: weights_from(): token_norm = jnp.sqrt(jnp.sum(values * values, axis=-1) + epsilon)]
  transfers between devices with their start and end apart: 1 -> 0, of which waited for: 1 -> 0; matrix products, arithmetic and copies ran while one was open for 0% -> 0% of each run, Pallas kernels for 0% -> 0%
where the time goes in v1:
time: 42.1 us; the launch traced here: 41.8 us
  blocking collectives  27.1 us (64%)
  Pallas kernels  12.7 us (30%)
  local copies, waits for them, and re-layouts  1.28 us (3%)
  between operations  0.66 us (2%)
    all_to_all x2, blocking collectives, exchange(): lax.all_to_all(pieces, ('section', 'expert'), split_axis=0, concat_axis=0...  27.1 us
    pallas_call x1, Pallas kernels, experts(): pl.pallas_call(lambda *refs: experts_kernel(*refs, chunk=chunk), out_shap...  7.57 us
    pallas_call x1, Pallas kernels, routing(): pl.pallas_call(lambda *refs: routing_kernel(*refs, sections=sections), ou...  2.79 us
    pallas_call x1, Pallas kernels, mixing(): pl.pallas_call(mixing_kernel, out_shape=jax.ShapeDtypeStruct(images.shape...  2.37 us
    broadcast_in_dim x1, local copies, waits for them, and re-layouts, local(): norm_gain[None, :]  1.28 us

profile of v1, /device:TPU:0, one launch (start us, length us, event | category | flops | bytes accessed | tf_op | source)
XLA Modules:
  0.0 41.8 jit_solution(14293932913633964208)
XLA Ops:
  0.7 1.3 %broadcast_in_dim.6.refs_2_ = bf16[1,1408]{1,0:T(2,128)(2,1)} reshape(bf16[1408]{0:T(1024)(128)(2,1)} %param.7) | data formatting | bytes 5632 | tf_op jit(solution)/shard_map/broadcast_in_dim | solution.py:154
  1.9 2.8 %routing.1 = (bf16[32,16,128]{2,1,0:T(8,128)(2,1)}, bf16[256,32]{1,0:T(8,128)(2,1)}) custom-call(f32[1]{0:T(128)S(6)} %copy.7.refs_0_, bf16[256,1408]{1,0:T(8,128)(2,1)} %bitcast.7, bf16[1,1408]{1,0:T(2,128)(2,1)} %broadcast_in_dim.6.refs_2_, bf16[16,1408]{1,0:T(8,128)(2,1)} %bitcast.9), custom_call_target="tpu_custom_call" | custom-call | tf_op jit(solution)/shard_map/routing/pallas_call | solution.py:63
  4.7 15.6 %all_to_all.10.refs_0_ = bf16[32,16,128]{2,1,0:T(8,128)(2,1)} all-to-all(bf16[32,16,128]{2,1,0:T(8,128)(2,1)} %get-tuple-element.8), channel_id=1, replica_groups=mesh['section'=2,'expert'=16] {'section','expert'}, dimensions={0} | all-to-all | bytes 262144 | tf_op jit(solution)/shard_map/all_to_all | solution.py:146
  20.4 7.6 %experts.1 = bf16[32,16,128]{2,1,0:T(8,128)(2,1)} custom-call(bf16[32,16,128]{2,1,0:T(8,128)(2,1)} %all_to_all.10.refs_0_, bf16[2560,1408]{1,0:T(8,128)(2,1)} %bitcast.5, bf16[2560,1408]{1,0:T(8,128)(2,1)} %bitcast.6), custom_call_target="tpu_custom_call" | custom-call | tf_op jit(solution)/shard_map/experts/pallas_call | solution.py:111
  27.9 11.5 %all_to_all.11.piece_ref = bf16[32,16,128]{2,1,0:T(8,128)(2,1)} all-to-all(bf16[32,16,128]{2,1,0:T(8,128)(2,1)} %experts.1), channel_id=1, replica_groups=mesh['section'=2,'expert'=16] {'section','expert'}, dimensions={0} | all-to-all | bytes 262144 | tf_op jit(solution)/shard_map/all_to_all | solution.py:146
  39.4 2.4 %mixing.1 = bf16[256,1408]{1,0:T(8,128)(2,1)} custom-call(bf16[256,1408]{1,0:T(8,128)(2,1)} %bitcast.8, bf16[256,32]{1,0:T(8,128)(2,1)} %get-tuple-element.7.combine_ref, bf16[32,16,128]{2,1,0:T(8,128)(2,1)} %all_to_all.11.piece_ref), custom_call_target="tpu_custom_call" | custom-call | tf_op jit(solution)/shard_map/mixing/pallas_call | solution.py:135

commit v2 on v1

v2 whole, which is shorter than its diff:
```python
import jax
import jax.numpy as jnp
from jax import lax
from jax.experimental import pallas as pl
from jax.experimental.pallas import tpu as pltpu
from jax.sharding import PartitionSpec as P

epsilon = 1e-06
LANES = 128
SCOPED = 12 * 2**20
f32 = jnp.float32
bf16 = jnp.bfloat16
NT = (((1,), (1,)), ((), ()))
TN = (((0,), (0,)), ((), ()))


def packed_rows(width):
    return -(-(width // LANES) // 16) * 16


def to_pieces(values, flat_ref, piece_ref, copies):
    count, width = values.shape
    rows = piece_ref.shape[1]
    flat_ref[...] = jnp.zeros(flat_ref.shape, f32)
    for j in range(width // LANES):
        flat_ref[pl.ds(j, count, stride=rows), :] = values[:, j * LANES : (j + 1) * LANES]
    pieces = flat_ref[...].astype(bf16).reshape(count, rows, LANES)
    for c in range(copies):
        piece_ref[c * count : (c + 1) * count] = pieces


def from_pieces(piece_ref, flat_ref, width):
    count, rows, _ = piece_ref.shape
    flat_ref[...] = piece_ref[...].reshape(count * rows, LANES).astype(f32)
    parts = [flat_ref[pl.ds(j, count, stride=rows), :] for j in range(width // LANES)]
    return jnp.concatenate(parts, axis=1).astype(bf16)


def gain_row(gain_ref):
    parts = [gain_ref[pl.ds(j, LANES)].astype(f32).reshape(1, LANES) for j in range(0, gain_ref.shape[0], LANES)]
    return jnp.concatenate(parts, axis=1)


def routing_kernel(
    scale_ref, images_hbm, gain_hbm, slots_hbm, piece_ref, combine_ref, *refs, sections, parts
):
    images_ref, gain_ref, slots_ref, normed_ref, flat_ref, sems = refs
    tokens = images_ref.shape[0]
    chunk = tokens // parts
    blocks = [pl.ds(i * chunk, chunk) for i in range(parts)]
    small = [
        pltpu.make_async_copy(gain_hbm, gain_ref, sems.at[0]),
        pltpu.make_async_copy(slots_hbm, slots_ref, sems.at[1]),
    ]
    loads = [
        pltpu.make_async_copy(images_hbm.at[block], images_ref.at[block], sems.at[2 + i])
        for i, block in enumerate(blocks)
    ]
    for copy in small + loads:
        copy.start()
    for copy in small:
        copy.wait()
    gain = gain_row(gain_ref)
    slot_rows = slots_ref[...]
    columns = slot_rows.astype(f32)
    column_norm = jnp.sqrt(jnp.sum(columns * columns, axis=-1, keepdims=True) + epsilon)
    column_row = jnp.transpose(jnp.broadcast_to(column_norm, (slot_rows.shape[0], LANES)))[:1, :]
    scores = []
    for block, load in zip(blocks, loads):
        load.wait()
        values = images_ref[block, :].astype(f32)
        spread = jnp.mean(values * values, axis=-1, keepdims=True)
        normed = (values * lax.rsqrt(spread + epsilon) * gain).astype(bf16)
        normed_ref[block, :] = normed
        raw = lax.dot_general(normed, slot_rows, NT, preferred_element_type=f32)
        wide = normed.astype(f32)
        token_norm = jnp.sqrt(jnp.sum(wide * wide, axis=-1, keepdims=True) + epsilon)
        scores.append(jnp.exp(scale_ref[0] * raw / (token_norm * column_row)))
    scores = jnp.concatenate(scores, axis=0)
    dispatch = (scores / jnp.sum(scores, axis=0, keepdims=True)).astype(bf16)
    slot_in = lax.dot_general(dispatch, normed_ref[...], TN, preferred_element_type=f32)
    to_pieces(slot_in, flat_ref, piece_ref, sections)
    combine = (scores / jnp.sum(scores, axis=1, keepdims=True)).astype(bf16)
    combine_ref[...] = jnp.concatenate([combine] * sections, axis=1)


def in_hbm(array):
    return pltpu.with_memory_space_constraint(array, pltpu.MemorySpace.HBM)


def in_vmem(array):
    return pltpu.with_memory_space_constraint(array, pltpu.MemorySpace.VMEM)


def routing(scale, images, gain, slot_rows, sections):
    tokens, width = images.shape
    count = slot_rows.shape[0]
    rows = packed_rows(width)
    parts = 4 if tokens % 64 == 0 else 1
    vmem = pl.BlockSpec(memory_space=pltpu.VMEM)
    hbm = pl.BlockSpec(memory_space=pltpu.MemorySpace.HBM)
    return pl.pallas_call(
        lambda *refs: routing_kernel(*refs, sections=sections, parts=parts),
        out_shape=(
            pltpu.VMEM((sections * count, rows, LANES), bf16),
            pltpu.VMEM((tokens, sections * count), bf16),
        ),
        in_specs=[pl.BlockSpec(memory_space=pltpu.SMEM)] + [hbm] * 3,
        out_specs=(vmem, vmem),
        scratch_shapes=[
            pltpu.VMEM(images.shape, bf16),
            pltpu.VMEM(gain.shape, bf16),
            pltpu.VMEM(slot_rows.shape, bf16),
            pltpu.VMEM(images.shape, bf16),
            pltpu.VMEM((count * rows, LANES), f32),
            pltpu.SemaphoreType.DMA((2 + parts,)),
        ],
        compiler_params=pltpu.CompilerParams(vmem_limit_bytes=SCOPED),
        cost_estimate=pl.CostEstimate(flops=10**10, bytes_accessed=10**8, transcendentals=0),
        name="routing",
    )(scale, in_hbm(images), in_hbm(gain), in_hbm(slot_rows))


def experts_kernel(piece_ref, up_ref, down_ref, out_ref, flat_ref, *, chunk):
    hidden_rows, width = up_ref.shape
    inputs = from_pieces(piece_ref, flat_ref, width)
    total = None
    for i in range(0, hidden_rows, chunk):
        block = pl.ds(i, chunk)
        hidden = lax.dot_general(inputs, up_ref[block, :], NT, preferred_element_type=f32)
        hidden = jax.nn.gelu(hidden).astype(bf16)
        term = jnp.dot(hidden, down_ref[block, :], preferred_element_type=f32)
        total = term if total is None else total + term
    to_pieces(total, flat_ref, out_ref, 1)


def experts(pieces, up, down, chunk):
    count, rows, _ = pieces.shape
    vmem = pl.BlockSpec(memory_space=pltpu.VMEM)
    return pl.pallas_call(
        lambda *refs: experts_kernel(*refs, chunk=chunk),
        out_shape=pltpu.VMEM(pieces.shape, bf16),
        in_specs=[vmem, vmem, vmem],
        out_specs=vmem,
        scratch_shapes=[pltpu.VMEM((count * rows, LANES), f32)],
        compiler_params=pltpu.CompilerParams(vmem_limit_bytes=SCOPED),
        name="experts",
    )(in_vmem(pieces), in_vmem(up), in_vmem(down))


def mixing_kernel(images_ref, combine_ref, piece_ref, out_hbm, flat_ref, out_ref, sems, *, chunk):
    tokens, width = images_ref.shape
    outputs = from_pieces(piece_ref, flat_ref, width)
    copies = []
    for i in range(tokens // chunk):
        part = pl.ds(i * chunk, chunk)
        mixed = jnp.dot(combine_ref[part, :], outputs, preferred_element_type=f32)
        out_ref[part, :] = (images_ref[part, :].astype(f32) + mixed).astype(bf16)
        copies.append(pltpu.make_async_copy(out_ref.at[part], out_hbm.at[part], sems.at[i]))
        copies[-1].start()
    for copy in copies:
        copy.wait()


def mixing(images, combine, pieces):
    count, rows, _ = pieces.shape
    tokens, width = images.shape
    chunk = tokens // 4 if tokens % 64 == 0 else tokens
    vmem = pl.BlockSpec(memory_space=pltpu.VMEM)
    return pl.pallas_call(
        lambda *refs: mixing_kernel(*refs, chunk=chunk),
        out_shape=jax.ShapeDtypeStruct(images.shape, bf16),
        in_specs=[vmem, vmem, vmem],
        out_specs=pl.BlockSpec(memory_space=pl.ANY),
        scratch_shapes=[
            pltpu.VMEM((count * rows, LANES), f32),
            pltpu.VMEM((tokens, width), bf16),
            pltpu.SemaphoreType.DMA((tokens // chunk,)),
        ],
        compiler_params=pltpu.CompilerParams(vmem_limit_bytes=SCOPED),
        name="mixing",
    )(in_vmem(images), in_vmem(combine), in_vmem(pieces))


def exchange(pieces):
    return lax.all_to_all(pieces, ("section", "expert"), split_axis=0, concat_axis=0, tiled=True)


def solution(mesh):
    sections = mesh.shape["section"]

    def local(images, norm_gain, slot_map, logit_scale, up_weight, down_weight):
        own, up, down = images[0], up_weight[0], down_weight[0]
        hidden_rows = up.shape[0]
        chunk = next(c for c in (512, 256, 128, hidden_rows) if hidden_rows % c == 0)
        pieces, combine = routing(logit_scale, own, norm_gain, slot_map.T, sections)
        arrived = exchange(pieces)
        results = experts(arrived, up, down, chunk)
        back = exchange(results)
        return mixing(own, combine, back)[None]

    return jax.shard_map(
        local,
        mesh=mesh,
        in_specs=(
            P(("section", "expert"), None, None),
            P(),
            P(),
            P(),
            P("expert", "section", None),
            P("expert", "section", None),
        ),
        out_specs=P(("section", "expert"), None, None),
        check_vma=False,
    )
```

time: 42.1 us -> 33.7 us (0.80)
  Pallas kernels: 12.7 us -> 7.52 us
  blocking collectives: 27.1 us -> 25.2 us
  local copies, waits for them, and re-layouts: 1.28 us -> 0.01 us
    pallas_call x1, Pallas kernels: 7.57 us -> 3.63 us  [experts(): pl.pallas_call(lambda *refs: experts_kernel(*refs, chunk=chunk), out_shap...]
    all_to_all x2, blocking collectives: 27.1 us -> 25.2 us  [exchange(): lax.all_to_all(pieces, ('section', 'expert'), split_axis=0, concat_axis=0...]
    broadcast_in_dim x1 -> x0, local copies, waits for them, and re-layouts: 1.28 us -> none  [local(): norm_gain[None, :]]
    pallas_call x2, Pallas kernels: 5.16 us -> 3.89 us  [the longest x1 2.79 us: routing(): pl.pallas_call(lambda *refs: routing_kernel(*refs, sections=sections, par...]
where the time goes in v2:
time: 33.7 us; the launch traced here: 33.5 us
  blocking collectives  25.2 us (75%)
  Pallas kernels  7.52 us (22%)
  between operations  0.69 us (2%)
    all_to_all x2, blocking collectives, exchange(): lax.all_to_all(pieces, ('section', 'expert'), split_axis=0, concat_axis=0...  25.2 us
    pallas_call x1, Pallas kernels, experts(): pl.pallas_call(lambda *refs: experts_kernel(*refs, chunk=chunk), out_shap...  3.63 us
    pallas_call x1, Pallas kernels, routing(): pl.pallas_call(lambda *refs: routing_kernel(*refs, sections=sections, par...  2.79 us
    pallas_call x1, Pallas kernels, mixing(): pl.pallas_call(lambda *refs: mixing_kernel(*refs, chunk=chunk), out_shape...  1.11 us

profile of v2, /device:TPU:0, one launch (start us, length us, event | category | flops | bytes accessed | tf_op | source)
XLA Modules:
  0.0 33.5 jit_solution(16056426176837761343)
XLA Ops:
  0.7 0.0 copy-start
  0.7 0.0 copy-start.1
  0.7 2.8 %routing.1 = (bf16[32,16,128]{2,1,0:T(8,128)(2,1)S(1)}, bf16[256,32]{1,0:T(8,128)(2,1)S(1)}) custom-call(f32[1]{0:T(128)S(6)} %copy.7.refs_0_, bf16[256,1408]{1,0:T(8,128)(2,1)} %bitcast.7, bf16[1408]{0:T(1024)(128)(2,1)} %refs_2_.1, bf16[16,1408]{1,0:T(8,128)(2,1)} %bitcast.9), custom_call_target="tpu_custom_call" | custom-call | flops 10000000000 | bytes 100000000 | tf_op jit(solution)/shard_map/routing/pallas_call | solution.py:102
  3.5 15.3 %all_to_all.10.refs_0_ = bf16[32,16,128]{2,1,0:T(8,128)(2,1)S(1)} all-to-all(bf16[32,16,128]{2,1,0:T(8,128)(2,1)S(1)} %get-tuple-element.8), channel_id=1, replica_groups=mesh['section'=2,'expert'=16] {'section','expert'}, dimensions={0} | all-to-all | bytes 262144 | tf_op jit(solution)/shard_map/all_to_all | solution.py:186
  18.8 0.0 copy-done
  18.8 0.0 copy-done.1
  18.8 0.0 copy-start.2
  18.8 3.6 %experts.1 = bf16[32,16,128]{2,1,0:T(8,128)(2,1)S(1)} custom-call(bf16[32,16,128]{2,1,0:T(8,128)(2,1)S(1)} %all_to_all.10.refs_0_, bf16[2560,1408]{1,0:T(8,128)(2,1)S(1)} %bitcast.5, bf16[2560,1408]{1,0:T(8,128)(2,1)S(1)} %bitcast.6), custom_call_target="tpu_custom_call" | custom-call | tf_op jit(solution)/shard_map/experts/pallas_call | solution.py:140
  22.5 9.9 %all_to_all.11.refs_2_ = bf16[32,16,128]{2,1,0:T(8,128)(2,1)S(1)} all-to-all(bf16[32,16,128]{2,1,0:T(8,128)(2,1)S(1)} %experts.1), channel_id=1, replica_groups=mesh['section'=2,'expert'=16] {'section','expert'}, dimensions={0} | all-to-all | bytes 262144 | tf_op jit(solution)/shard_map/all_to_all | solution.py:186
  32.4 0.0 copy-done.2
  32.4 1.1 %mixing.1 = bf16[256,1408]{1,0:T(8,128)(2,1)} custom-call(bf16[256,1408]{1,0:T(8,128)(2,1)S(1)} %bitcast.8, bf16[256,32]{1,0:T(8,128)(2,1)S(1)} %get-tuple-element.7.refs_1_, bf16[32,16,128]{2,1,0:T(8,128)(2,1)S(1)} %all_to_all.11.refs_2_), custom_call_target="tpu_custom_call" | custom-call | tf_op jit(solution)/shard_map/mixing/pallas_call | solution.py:170
Async XLA Ops:
  0.7 18.2 %copy-start = (bf16[1,2560,1408]{2,1,0:T(8,128)(2,1)S(1)}, bf16[1,2560,1408]{2,1,0:T(8,128)(2,1)}, u32[]{:S(2)}) copy-start(bf16[1,2560,1408]{2,1,0:T(8,128)(2,1)} %param.10) | copy-start | bytes 21626884
  0.7 18.1 %copy-start.1 = (bf16[1,2560,1408]{2,1,0:T(8,128)(2,1)S(1)}, bf16[1,2560,1408]{2,1,0:T(8,128)(2,1)}, u32[]{:S(2)}) copy-start(bf16[1,2560,1408]{2,1,0:T(8,128)(2,1)} %param.11) | copy-start | bytes 21626884
  18.8 13.6 %copy-start.2 = (bf16[1,256,1408]{2,1,0:T(8,128)(2,1)S(1)}, bf16[1,256,1408]{2,1,0:T(8,128)(2,1)}, u32[]{:S(2)}) copy-start(bf16[1,256,1408]{2,1,0:T(8,128)(2,1)} %param.6) | copy-start | bytes 2162692

commit v3 on v2

--- a/solution.py
+++ b/solution.py
@@ -7,6 +7,7 @@
 
 epsilon = 1e-06
 LANES = 128
+SUB = 4
 SCOPED = 12 * 2**20
 f32 = jnp.float32
 bf16 = jnp.bfloat16
@@ -15,23 +16,25 @@
 
 
 def packed_rows(width):
-    return -(-(width // LANES) // 16) * 16
+    return -(-(width // LANES) // SUB) * SUB
 
 
 def to_pieces(values, flat_ref, piece_ref, copies):
     count, width = values.shape
-    rows = piece_ref.shape[1]
+    rows = packed_rows(width)
     flat_ref[...] = jnp.zeros(flat_ref.shape, f32)
     for j in range(width // LANES):
         flat_ref[pl.ds(j, count, stride=rows), :] = values[:, j * LANES : (j + 1) * LANES]
-    pieces = flat_ref[...].astype(bf16).reshape(count, rows, LANES)
+    groups = count * rows // SUB
+    pieces = flat_ref[...].reshape(groups, SUB, LANES).astype(bf16)
     for c in range(copies):
-        piece_ref[c * count : (c + 1) * count] = pieces
+        piece_ref[c * groups : (c + 1) * groups] = pieces
 
 
 def from_pieces(piece_ref, flat_ref, width):
-    count, rows, _ = piece_ref.shape
-    flat_ref[...] = piece_ref[...].reshape(count * rows, LANES).astype(f32)
+    rows = packed_rows(width)
+    count = piece_ref.shape[0] * SUB // rows
+    flat_ref[...] = piece_ref[...].astype(f32).reshape(count * rows, LANES)
     parts = [flat_ref[pl.ds(j, count, stride=rows), :] for j in range(width // LANES)]
     return jnp.concatenate(parts, axis=1).astype(bf16)
 
@@ -96,13 +99,13 @@
     tokens, width = images.shape
     count = slot_rows.shape[0]
     rows = packed_rows(width)
-    parts = 4 if tokens % 64 == 0 else 1
+    parts = 2 if tokens % 32 == 0 else 1
     vmem = pl.BlockSpec(memory_space=pltpu.VMEM)
     hbm = pl.BlockSpec(memory_space=pltpu.MemorySpace.HBM)
     return pl.pallas_call(
         lambda *refs: routing_kernel(*refs, sections=sections, parts=parts),
         out_shape=(
-            pltpu.VMEM((sections * count, rows, LANES), bf16),
+            pltpu.VMEM((sections * count * rows // SUB, SUB, LANES), bf16),
             pltpu.VMEM((tokens, sections * count), bf16),
         ),
         in_specs=[pl.BlockSpec(memory_space=pltpu.SMEM)] + [hbm] * 3,
@@ -135,7 +138,8 @@
 
 
 def experts(pieces, up, down, chunk):
-    count, rows, _ = pieces.shape
+    count = pieces.shape[0]
+    rows = SUB
     vmem = pl.BlockSpec(memory_space=pltpu.VMEM)
     return pl.pallas_call(
         lambda *refs: experts_kernel(*refs, chunk=chunk),
@@ -163,7 +167,8 @@
 
 
 def mixing(images, combine, pieces):
-    count, rows, _ = pieces.shape
+    count = pieces.shape[0]
+    rows = SUB
     tokens, width = images.shape
     chunk = tokens // 4 if tokens % 64 == 0 else tokens
     vmem = pl.BlockSpec(memory_space=pltpu.VMEM)
@@ -192,7 +197,7 @@
     def local(images, norm_gain, slot_map, logit_scale, up_weight, down_weight):
         own, up, down = images[0], up_weight[0], down_weight[0]
         hidden_rows = up.shape[0]
-        chunk = next(c for c in (512, 256, 128, hidden_rows) if hidden_rows % c == 0)
+        chunk = next(c for c in (1280, 640, hidden_rows) if hidden_rows % c == 0)
         pieces, combine = routing(logit_scale, own, norm_gain, slot_map.T, sections)
         arrived = exchange(pieces)
         results = experts(arrived, up, down, chunk)

time: 33.7 us -> 32 us (0.950)
  blocking collectives: 25.2 us -> 24.4 us
  Pallas kernels: 7.52 us -> 6.73 us
    all_to_all x2, blocking collectives: 25.2 us -> 24.4 us  [exchange(): lax.all_to_all(pieces, ('section', 'expert'), split_axis=0, concat_axis=0...]
    pallas_call x1, Pallas kernels: 2.79 us -> 2.35 us  [routing(): pl.pallas_call(lambda *refs: routing_kernel(*refs, sections=sections, par...]
    pallas_call x1, Pallas kernels: 3.63 us -> 3.28 us  [experts(): pl.pallas_call(lambda *refs: experts_kernel(*refs, chunk=chunk), out_shap...]
where the time goes in v3:
time: 32 us; the launch traced here: 31.8 us
  blocking collectives  24.4 us (76%)
  Pallas kernels  6.73 us (21%)
  between operations  0.69 us (2%)
    all_to_all x2, blocking collectives, exchange(): lax.all_to_all(pieces, ('section', 'expert'), split_axis=0, concat_axis=0...  24.4 us
    pallas_call x1, Pallas kernels, experts(): pl.pallas_call(lambda *refs: experts_kernel(*refs, chunk=chunk), out_shap...  3.28 us
    pallas_call x1, Pallas kernels, routing(): pl.pallas_call(lambda *refs: routing_kernel(*refs, sections=sections, par...  2.35 us
    pallas_call x1, Pallas kernels, mixing(): pl.pallas_call(lambda *refs: mixing_kernel(*refs, chunk=chunk), out_shape...  1.1 us

profile of v3, /device:TPU:0, one launch (start us, length us, event | category | flops | bytes accessed | tf_op | source)
XLA Modules:
  0.0 31.8 jit_solution(17246495325856283507)
XLA Ops:
  0.7 0.0 copy-start
  0.7 0.0 copy-start.1
  0.7 2.4 %routing.1 = (bf16[96,4,128]{2,1,0:T(4,128)(2,1)S(1)}, bf16[256,32]{1,0:T(8,128)(2,1)S(1)}) custom-call(f32[1]{0:T(128)S(6)} %copy.7.refs_0_, bf16[256,1408]{1,0:T(8,128)(2,1)} %bitcast.7, bf16[1408]{0:T(1024)(128)(2,1)} %refs_2_.1, bf16[16,1408]{1,0:T(8,128)(2,1)} %bitcast.9), custom_call_target="tpu_custom_call" | custom-call | flops 10000000000 | bytes 100000000 | tf_op jit(solution)/shard_map/routing/pallas_call | solution.py:105
  3.0 14.9 %all_to_all.10.refs_0_ = bf16[96,4,128]{2,1,0:T(4,128)(2,1)S(1)} all-to-all(bf16[96,4,128]{2,1,0:T(4,128)(2,1)S(1)} %get-tuple-element.8), channel_id=1, replica_groups=mesh['section'=2,'expert'=16] {'section','expert'}, dimensions={0} | all-to-all | bytes 196608 | tf_op jit(solution)/shard_map/all_to_all | solution.py:191
  18.0 0.0 copy-done
  18.0 0.0 copy-done.1
  18.0 0.0 copy-start.2
  18.0 3.3 %experts.1 = bf16[96,4,128]{2,1,0:T(4,128)(2,1)S(1)} custom-call(bf16[96,4,128]{2,1,0:T(4,128)(2,1)S(1)} %all_to_all.10.refs_0_, bf16[2560,1408]{1,0:T(8,128)(2,1)S(1)} %bitcast.5, bf16[2560,1408]{1,0:T(8,128)(2,1)S(1)} %bitcast.6), custom_call_target="tpu_custom_call" | custom-call | tf_op jit(solution)/shard_map/experts/pallas_call | solution.py:144
  21.2 9.5 %all_to_all.11.refs_2_ = bf16[96,4,128]{2,1,0:T(4,128)(2,1)S(1)} all-to-all(bf16[96,4,128]{2,1,0:T(4,128)(2,1)S(1)} %experts.1), channel_id=1, replica_groups=mesh['section'=2,'expert'=16] {'section','expert'}, dimensions={0} | all-to-all | bytes 196608 | tf_op jit(solution)/shard_map/all_to_all | solution.py:191
  30.7 0.0 copy-done.2
  30.7 1.1 %mixing.1 = bf16[256,1408]{1,0:T(8,128)(2,1)} custom-call(bf16[256,1408]{1,0:T(8,128)(2,1)S(1)} %bitcast.8, bf16[256,32]{1,0:T(8,128)(2,1)S(1)} %get-tuple-element.7.refs_1_, bf16[96,4,128]{2,1,0:T(4,128)(2,1)S(1)} %all_to_all.11.refs_2_), custom_call_target="tpu_custom_call" | custom-call | tf_op jit(solution)/shard_map/mixing/pallas_call | solution.py:175
Async XLA Ops:
  0.7 17.3 %copy-start = (bf16[1,2560,1408]{2,1,0:T(8,128)(2,1)S(1)}, bf16[1,2560,1408]{2,1,0:T(8,128)(2,1)}, u32[]{:S(2)}) copy-start(bf16[1,2560,1408]{2,1,0:T(8,128)(2,1)} %param.10) | copy-start | bytes 21626884
  0.7 17.3 %copy-start.1 = (bf16[1,2560,1408]{2,1,0:T(8,128)(2,1)S(1)}, bf16[1,2560,1408]{2,1,0:T(8,128)(2,1)}, u32[]{:S(2)}) copy-start(bf16[1,2560,1408]{2,1,0:T(8,128)(2,1)} %param.11) | copy-start | bytes 21626884
  18.0 12.8 %copy-start.2 = (bf16[1,256,1408]{2,1,0:T(8,128)(2,1)S(1)}, bf16[1,256,1408]{2,1,0:T(8,128)(2,1)}, u32[]{:S(2)}) copy-start(bf16[1,256,1408]{2,1,0:T(8,128)(2,1)} %param.6) | copy-start | bytes 2162692
